TPU v7x, 32 devices: a whole 2x2x4 slice. The times are simulated.
32 devices in a mesh: member: 8 (over y, x, core), strip: 4 (over z).
Axes of the slice: x: 2, y: 2, z: 4, core: 2. Of those that a mesh axis runs over, the one named last changes fastest.
Arguments:
- sample_fields: float32 [64, 3, 64, 1024], P('member', None, 'strip'), may hold values from -0.8 to 0.8
- report_counts: int32 [4, 8], P('strip', 'member'), may hold values from 1 to 256, as said below
- report_cells: int32 [4, 8, 256], P('strip', 'member'), may hold values from 0 to 2047
- report_values: float32 [4, 8, 256], P('strip', 'member'), may hold values from -1.5 to 1.5
- report_errors: float32 [4, 8, 256], P('strip', 'member'), may hold values from 0.04 to 0.2
- local_radius: int32 [4, 8], P('strip', 'member'), may hold values from 1 to 3
Outputs:
- analysis: float32 [64, 3, 64, 1024], P('member', None, 'strip')
Inputs may be any that keep to these rules, and one draw needn't show every extreme that they name: `report_counts`: counts lie between 1 and 256; 256 is reached by some region in every draw; slots from the count on are not used.
All inputs are finite; a program needn't handle non-finite values.
Results may differ from a plain program's by a relative error of at most 0.0003.
Values sent between devices are 32-bit elements; how exact they have to be, the bound alone decides.
No kernel may reach another device: no remote copies, remote signals or barrier semaphores. Data moves between devices by JAX's collectives and lax.ppermute only.
A program may use at most 64 MiB of HBM per device.

v0:
```python
import jax
import jax.numpy as jnp
from jax import lax
from jax.sharding import PartitionSpec as P

BAND_HEIGHT_CELLS = 16
PATCH_WIDTH_CELLS = 128
STEPS = 12
TURNS = 20
COURANT = 0.125
GRAVITY = 1.0
ROTATION = 0.05
HIGHEST_PRECISION = lax.Precision.HIGHEST


def with_halo(block, sides, width):
    for axis, dim in sides:
        count = lax.axis_size(axis)
        forward = [(i, i + 1) for i in range(count - 1)]
        forward.append((count - 1, 0))
        backward = [(target, source) for source, target in forward]
        low = lax.ppermute(
            lax.slice_in_dim(block, block.shape[dim] - width, None, axis=dim), axis, forward
        )
        high = lax.ppermute(lax.slice_in_dim(block, 0, width, axis=dim), axis, backward)
        block = jnp.concatenate([low, block, high], axis=dim)
    return block


def to_east(field):
    return field[..., 1:-1, 2:]


def to_west(field):
    return field[..., 1:-1, :-2]


def to_north(field):
    return field[..., 2:, 1:-1]


def to_south(field):
    return field[..., :-2, 1:-1]


def middle(field):
    return field[..., 1:-1, 1:-1]


def neighbour_mean(field):
    return 0.25 * (to_east(field) + to_west(field) + to_north(field) + to_south(field))


def advance_once(padded):
    height = padded[:, 0]
    flow_x = padded[:, 1]
    flow_y = padded[:, 2]
    column_depth = 1.0 + height
    flux_x = column_depth * flow_x
    flux_y = column_depth * flow_y
    centre_x = middle(flow_x)
    centre_y = middle(flow_y)
    new_height = neighbour_mean(height) - COURANT * (
        to_east(flux_x) - to_west(flux_x) + to_north(flux_y) - to_south(flux_y)
    )
    new_flow_x = (
        neighbour_mean(flow_x)
        - COURANT
        * (
            centre_x * (to_east(flow_x) - to_west(flow_x))
            + centre_y * (to_north(flow_x) - to_south(flow_x))
            + GRAVITY * (to_east(height) - to_west(height))
        )
        + ROTATION * centre_y
    )
    new_flow_y = (
        neighbour_mean(flow_y)
        - COURANT
        * (
            centre_x * (to_east(flow_y) - to_west(flow_y))
            + centre_y * (to_north(flow_y) - to_south(flow_y))
            + GRAVITY * (to_north(height) - to_south(height))
        )
        - ROTATION * centre_x
    )
    return jnp.stack([new_height, new_flow_x, new_flow_y], axis=1)


def observe(region, locations, values, errors, live_count):
    observed = jnp.take(region, locations, axis=1)
    observed_mean = jnp.mean(observed, axis=0)
    spread = observed - observed_mean[None, :]
    innovation = values - observed_mean
    slot_ids = jnp.arange(locations.shape[0])
    precision = jnp.where(slot_ids < live_count, 1.0 / errors, 0.0 * errors)
    row_pos = ((locations // PATCH_WIDTH_CELLS).astype(jnp.float32) + 0.5) / BAND_HEIGHT_CELLS - 0.5
    col_pos = ((locations % PATCH_WIDTH_CELLS).astype(jnp.float32) + 0.5) / PATCH_WIDTH_CELLS - 0.5
    return jnp.concatenate(
        [spread, innovation[None], precision[None], row_pos[None], col_pos[None]], axis=0
    )


def analyse(region, neighbours, radius_blocks):
    sample_collection = region.shape[0]
    offsets = jnp.arange(3).astype(region.dtype) - 1.0
    anomalies = neighbours[:, :, :sample_collection, :]
    innovation = neighbours[:, :, sample_collection, :].reshape(-1)
    precision = neighbours[:, :, sample_collection + 1, :]
    row_pos = neighbours[:, :, sample_collection + 2, :] + offsets[:, None, None]
    col_pos = neighbours[:, :, sample_collection + 3, :] + offsets[None, :, None]
    radius_float = radius_blocks.astype(region.dtype)
    tapering = jnp.exp(
        -0.5 * (row_pos * row_pos + col_pos * col_pos) / (radius_float * radius_float)
    )
    weights = (tapering * precision).reshape(-1)
    spread = jnp.transpose(anomalies, (2, 0, 1, 3)).reshape(sample_collection, -1)
    weighted = spread * weights[None, :]
    ensemble_scale = sample_collection - 1.0
    identity = jnp.eye(sample_collection, dtype=region.dtype)
    gram_matrix = jnp.dot(weighted, spread.T, precision=HIGHEST_PRECISION)
    normal = identity + gram_matrix / ensemble_scale
    pull_vector = jnp.dot(weighted, innovation, precision=HIGHEST_PRECISION)
    frob_norm = jnp.sqrt(jnp.sum(normal * normal))
    iterate = normal / frob_norm
    inverse_root = identity
    for newton_turn in range(TURNS):
        factor = 1.5 * identity - 0.5 * jnp.dot(inverse_root, iterate, precision=HIGHEST_PRECISION)
        iterate = jnp.dot(iterate, factor, precision=HIGHEST_PRECISION)
        inverse_root = jnp.dot(factor, inverse_root, precision=HIGHEST_PRECISION)
    root_inverse = inverse_root / jnp.sqrt(frob_norm)
    full_inverse = jnp.dot(inverse_root, inverse_root, precision=HIGHEST_PRECISION) / frob_norm
    mean_weights = jnp.dot(full_inverse, pull_vector, precision=HIGHEST_PRECISION) / ensemble_scale
    transform = root_inverse + mean_weights[:, None]
    centre = jnp.mean(region, axis=0)
    deviations = region - centre[None, :]
    return centre[None, :] + jnp.dot(transform.T, deviations, precision=HIGHEST_PRECISION)


def strip_block(current_state, halo_depth):
    padded = with_halo(current_state, (("strip", 2),), halo_depth)
    padded = jnp.concatenate([padded[..., -halo_depth:], padded, padded[..., :halo_depth]], axis=3)
    for repeat in range(halo_depth):
        padded = advance_once(padded)
    return padded


def on_device(
    sample_fields, report_counts, report_cells, report_values, report_errors, local_radius
):
    own_members, fields, row_count, grid_cols = sample_fields.shape
    blocks = lax.axis_size("member")
    region_cols = grid_cols // blocks
    sample_collection = own_members * blocks
    halo_depth = 3
    rounds = STEPS // halo_depth

    def strip_round(counter, carried):
        return strip_block(carried, halo_depth)

    current_state = lax.fori_loop(0, rounds, strip_round, sample_fields)
    by_block = current_state.reshape(own_members, fields, row_count, blocks, region_cols)
    current_state = lax.all_to_all(by_block, "member", split_axis=3, concat_axis=0, tiled=True)
    region = current_state.reshape(sample_collection, fields * row_count * region_cols)
    packed = observe(
        region, report_cells[0, 0], report_values[0, 0], report_errors[0, 0], report_counts[0, 0]
    )
    neighbours = with_halo(packed[None, None], (("member", 1), ("strip", 0)), 1)
    updated = analyse(region, neighbours, local_radius[0, 0])
    outgoing = updated.reshape(sample_collection, fields, row_count, 1, region_cols)
    returned = lax.all_to_all(outgoing, "member", split_axis=0, concat_axis=3, tiled=True)
    return returned.reshape(own_members, fields, row_count, grid_cols)


def solution(mesh):
    in_specs = (
        P("member", None, "strip", None),
        P("strip", "member"),
        P("strip", "member", None),
        P("strip", "member", None),
        P("strip", "member", None),
        P("strip", "member"),
    )
    out_specs = P("member", None, "strip", None)
    return jax.shard_map(
        on_device, mesh=mesh, in_specs=in_specs, out_specs=out_specs, check_vma=False
    )
```

profile of v0, /device:TPU:0, one launch (start us, length us, event | category | flops | bytes accessed | tf_op | source)
XLA Modules:
  0.0 245.0 jit_solution(7391086606007713092)
XLA Ops:
  1.5 151.1 %while.10 = (s32[]{:T(128)}, f32[8,3,16,1024]{3,2,0,1:T(8,128)S(1)}, s32[]{:T(128)}) while((s32[]{:T(128)}, f32[8,3,16,1024]{3,2,0,1:T(8,128)S(1)}, s32[]{:T(128)}) %tuple.56), condition=%wide.region_1.0_spmd, body=%wide.region_0.0_spmd.sunk | while | flops 20949056 | bytes 80089624 | solution.py:160
  1.7 5.1 %collective-permute-start = (f32[8,3,3,1024]{3,2,0,1:T(4,128)S(1)}, f32[8,3,3,1024]{3,2,0,1:T(4,128)S(1)}, u32[]{:S(2)}, u32[]{:S(2)}) collective-permute-start(f32[8,3,3,1024]{3,2,0,1:T(4,128)S(1)} %get-tuple-element.91), channel_id=1, source_target_pairs={{1,0},{2,1},{3,2},{0,3},{5,4},{6,5},{7,6},{4,7},{9,8},{10,9},{11,1... | collective-permute-start | bytes 884744 | tf_op jit(solution)/shard_map/while/body/eval_jaxpr/ppermute | solution.py:25
  6.8 9.5 %collective-permute-done = f32[8,3,3,1024]{3,2,0,1:T(4,128)S(1)} collective-permute-done((f32[8,3,3,1024]{3,2,0,1:T(4,128)S(1)}, f32[8,3,3,1024]{3,2,0,1:T(4,128)S(1)}, u32[]{:S(2)}, u32[]{:S(2)}) %collective-permute-start) | collective-permute-done | bytes 294944 | tf_op jit(solution)/shard_map/while/body/eval_jaxpr/ppermute | solution.py:25
  16.3 8.2 %collective-permute-done.1 = f32[8,3,3,1024]{3,2,0,1:T(4,128)S(1)} collective-permute-done((f32[8,3,3,1024]{3,2,0,1:T(4,128)S(1)}, f32[8,3,3,1024]{3,2,0,1:T(4,128)S(1)}, u32[]{:S(2)}, u32[]{:S(2)}) %collective-permute-start.1) | collective-permute-done | bytes 294944 | tf_op jit(solution)/shard_map/while/body/eval_jaxpr/ppermute | solution.py:22
  26.4 3.2 %concatenate.19 = f32[8,3,22,1030]{3,2,0,1:T(8,128)S(1)} concatenate(f32[8,3,22,3]{3,2,0,1:T(8,128)S(1)} %get-tuple-element.93, f32[8,3,22,1024]{3,2,0,1:T(8,128)} %copy-done, f32[8,3,22,3]{3,2,0,1:T(8,128)S(1)} %get-tuple-element.94), dimensions={3} | concatenate | bytes 4350720 | tf_op jit(solution)/shard_map/while/body/eval_jaxpr/concatenate | solution.py:141
  29.9 2.8 %add_multiply_fusion.12 = (f32[8,20,1028]{2,1,0:T(8,128)S(1)}, f32[8,20,1028]{2,1,0:T(8,128)S(1)}, f32[8,20,1028]{2,1,0:T(8,128)S(1)}) fusion(f32[8,22,1030]{2,1,0:T(8,128)S(1)} %get-tuple-element.95, f32[8,22,1030]{2,1,0:T(8,128)S(1)} %get-tuple-element.96, f32[8,22,1030]{2,1,0:T(8,128)S(1)} %get-tuple-element.97, ...), kind=kLoop, calls=%fused_computation.23.clone.1 | loop fusion | flops 4276480 | bytes 11184640 | tf_op jit(solution)/shard_map/while/body/eval_jaxpr/mul | solution.py:59
  34.4 2.8 %add_multiply_fusion.14 = (f32[8,18,1026]{2,1,0:T(8,128)S(1)}, f32[8,18,1026]{2,1,0:T(8,128)S(1)}, f32[8,18,1026]{2,1,0:T(8,128)S(1)}) fusion(f32[8,20,1028]{2,1,0:T(8,128)S(1)} %get-tuple-element.101, f32[8,20,1028]{2,1,0:T(8,128)S(1)} %get-tuple-element.102, f32[8,20,1028]{2,1,0:T(8,128)S(1)} %get-tuple-element.100, ...), kind=kLoop, calls=%fused_computation.21.clone.1 | loop fusion | flops 3841344 | bytes 10046592 | tf_op jit(solution)/shard_map/while/body/eval_jaxpr/mul | solution.py:59
  43.8 16.4 %collective-permute-done = f32[8,3,3,1024]{3,2,0,1:T(4,128)S(1)} collective-permute-done((f32[8,3,3,1024]{3,2,0,1:T(4,128)S(1)}, f32[8,3,3,1024]{3,2,0,1:T(4,128)S(1)}, u32[]{:S(2)}, u32[]{:S(2)}) %collective-permute-start) | collective-permute-done | bytes 294944 | tf_op jit(solution)/shard_map/while/body/eval_jaxpr/ppermute | solution.py:25
  62.1 3.2 %concatenate.19 = f32[8,3,22,1030]{3,2,0,1:T(8,128)S(1)} concatenate(f32[8,3,22,3]{3,2,0,1:T(8,128)S(1)} %get-tuple-element.93, f32[8,3,22,1024]{3,2,0,1:T(8,128)} %copy-done, f32[8,3,22,3]{3,2,0,1:T(8,128)S(1)} %get-tuple-element.94), dimensions={3} | concatenate | bytes 4350720 | tf_op jit(solution)/shard_map/while/body/eval_jaxpr/concatenate | solution.py:141
  65.7 2.8 %add_multiply_fusion.12 = (f32[8,20,1028]{2,1,0:T(8,128)S(1)}, f32[8,20,1028]{2,1,0:T(8,128)S(1)}, f32[8,20,1028]{2,1,0:T(8,128)S(1)}) fusion(f32[8,22,1030]{2,1,0:T(8,128)S(1)} %get-tuple-element.95, f32[8,22,1030]{2,1,0:T(8,128)S(1)} %get-tuple-element.96, f32[8,22,1030]{2,1,0:T(8,128)S(1)} %get-tuple-element.97, ...), kind=kLoop, calls=%fused_computation.23.clone.1 | loop fusion | flops 4276480 | bytes 11184640 | tf_op jit(solution)/shard_map/while/body/eval_jaxpr/mul | solution.py:59
  70.1 2.8 %add_multiply_fusion.14 = (f32[8,18,1026]{2,1,0:T(8,128)S(1)}, f32[8,18,1026]{2,1,0:T(8,128)S(1)}, f32[8,18,1026]{2,1,0:T(8,128)S(1)}) fusion(f32[8,20,1028]{2,1,0:T(8,128)S(1)} %get-tuple-element.101, f32[8,20,1028]{2,1,0:T(8,128)S(1)} %get-tuple-element.102, f32[8,20,1028]{2,1,0:T(8,128)S(1)} %get-tuple-element.100, ...), kind=kLoop, calls=%fused_computation.21.clone.1 | loop fusion | flops 3841344 | bytes 10046592 | tf_op jit(solution)/shard_map/while/body/eval_jaxpr/mul | solution.py:59
  77.5 2.6 %collective-permute-start = (f32[8,3,3,1024]{3,2,0,1:T(4,128)S(1)}, f32[8,3,3,1024]{3,2,0,1:T(4,128)S(1)}, u32[]{:S(2)}, u32[]{:S(2)}) collective-permute-start(f32[8,3,3,1024]{3,2,0,1:T(4,128)S(1)} %get-tuple-element.91), channel_id=1, source_target_pairs={{1,0},{2,1},{3,2},{0,3},{5,4},{6,5},{7,6},{4,7},{9,8},{10,9},{11,1... | collective-permute-start | bytes 884744 | tf_op jit(solution)/shard_map/while/body/eval_jaxpr/ppermute | solution.py:25
  80.1 9.5 %collective-permute-done = f32[8,3,3,1024]{3,2,0,1:T(4,128)S(1)} collective-permute-done((f32[8,3,3,1024]{3,2,0,1:T(4,128)S(1)}, f32[8,3,3,1024]{3,2,0,1:T(4,128)S(1)}, u32[]{:S(2)}, u32[]{:S(2)}) %collective-permute-start) | collective-permute-done | bytes 294944 | tf_op jit(solution)/shard_map/while/body/eval_jaxpr/ppermute | solution.py:25
  89.6 9.2 %collective-permute-done.1 = f32[8,3,3,1024]{3,2,0,1:T(4,128)S(1)} collective-permute-done((f32[8,3,3,1024]{3,2,0,1:T(4,128)S(1)}, f32[8,3,3,1024]{3,2,0,1:T(4,128)S(1)}, u32[]{:S(2)}, u32[]{:S(2)}) %collective-permute-start.1) | collective-permute-done | bytes 294944 | tf_op jit(solution)/shard_map/while/body/eval_jaxpr/ppermute | solution.py:22
  100.6 3.2 %concatenate.19 = f32[8,3,22,1030]{3,2,0,1:T(8,128)S(1)} concatenate(f32[8,3,22,3]{3,2,0,1:T(8,128)S(1)} %get-tuple-element.93, f32[8,3,22,1024]{3,2,0,1:T(8,128)} %copy-done, f32[8,3,22,3]{3,2,0,1:T(8,128)S(1)} %get-tuple-element.94), dimensions={3} | concatenate | bytes 4350720 | tf_op jit(solution)/shard_map/while/body/eval_jaxpr/concatenate | solution.py:141
  104.2 2.8 %add_multiply_fusion.12 = (f32[8,20,1028]{2,1,0:T(8,128)S(1)}, f32[8,20,1028]{2,1,0:T(8,128)S(1)}, f32[8,20,1028]{2,1,0:T(8,128)S(1)}) fusion(f32[8,22,1030]{2,1,0:T(8,128)S(1)} %get-tuple-element.95, f32[8,22,1030]{2,1,0:T(8,128)S(1)} %get-tuple-element.96, f32[8,22,1030]{2,1,0:T(8,128)S(1)} %get-tuple-element.97, ...), kind=kLoop, calls=%fused_computation.23.clone.1 | loop fusion | flops 4276480 | bytes 11184640 | tf_op jit(solution)/shard_map/while/body/eval_jaxpr/mul | solution.py:59
  108.7 2.8 %add_multiply_fusion.14 = (f32[8,18,1026]{2,1,0:T(8,128)S(1)}, f32[8,18,1026]{2,1,0:T(8,128)S(1)}, f32[8,18,1026]{2,1,0:T(8,128)S(1)}) fusion(f32[8,20,1028]{2,1,0:T(8,128)S(1)} %get-tuple-element.101, f32[8,20,1028]{2,1,0:T(8,128)S(1)} %get-tuple-element.102, f32[8,20,1028]{2,1,0:T(8,128)S(1)} %get-tuple-element.100, ...), kind=kLoop, calls=%fused_computation.21.clone.1 | loop fusion | flops 3841344 | bytes 10046592 | tf_op jit(solution)/shard_map/while/body/eval_jaxpr/mul | solution.py:59
  118.1 9.2 %collective-permute-done = f32[8,3,3,1024]{3,2,0,1:T(4,128)S(1)} collective-permute-done((f32[8,3,3,1024]{3,2,0,1:T(4,128)S(1)}, f32[8,3,3,1024]{3,2,0,1:T(4,128)S(1)}, u32[]{:S(2)}, u32[]{:S(2)}) %collective-permute-start) | collective-permute-done | bytes 294944 | tf_op jit(solution)/shard_map/while/body/eval_jaxpr/ppermute | solution.py:25
  127.3 8.1 %collective-permute-done.1 = f32[8,3,3,1024]{3,2,0,1:T(4,128)S(1)} collective-permute-done((f32[8,3,3,1024]{3,2,0,1:T(4,128)S(1)}, f32[8,3,3,1024]{3,2,0,1:T(4,128)S(1)}, u32[]{:S(2)}, u32[]{:S(2)}) %collective-permute-start.1) | collective-permute-done | bytes 294944 | tf_op jit(solution)/shard_map/while/body/eval_jaxpr/ppermute | solution.py:22
  137.2 3.2 %concatenate.19 = f32[8,3,22,1030]{3,2,0,1:T(8,128)S(1)} concatenate(f32[8,3,22,3]{3,2,0,1:T(8,128)S(1)} %get-tuple-element.93, f32[8,3,22,1024]{3,2,0,1:T(8,128)} %copy-done, f32[8,3,22,3]{3,2,0,1:T(8,128)S(1)} %get-tuple-element.94), dimensions={3} | concatenate | bytes 4350720 | tf_op jit(solution)/shard_map/while/body/eval_jaxpr/concatenate | solution.py:141
  140.8 2.8 %add_multiply_fusion.12 = (f32[8,20,1028]{2,1,0:T(8,128)S(1)}, f32[8,20,1028]{2,1,0:T(8,128)S(1)}, f32[8,20,1028]{2,1,0:T(8,128)S(1)}) fusion(f32[8,22,1030]{2,1,0:T(8,128)S(1)} %get-tuple-element.95, f32[8,22,1030]{2,1,0:T(8,128)S(1)} %get-tuple-element.96, f32[8,22,1030]{2,1,0:T(8,128)S(1)} %get-tuple-element.97, ...), kind=kLoop, calls=%fused_computation.23.clone.1 | loop fusion | flops 4276480 | bytes 11184640 | tf_op jit(solution)/shard_map/while/body/eval_jaxpr/mul | solution.py:59
  145.3 2.8 %add_multiply_fusion.14 = (f32[8,18,1026]{2,1,0:T(8,128)S(1)}, f32[8,18,1026]{2,1,0:T(8,128)S(1)}, f32[8,18,1026]{2,1,0:T(8,128)S(1)}) fusion(f32[8,20,1028]{2,1,0:T(8,128)S(1)} %get-tuple-element.101, f32[8,20,1028]{2,1,0:T(8,128)S(1)} %get-tuple-element.102, f32[8,20,1028]{2,1,0:T(8,128)S(1)} %get-tuple-element.100, ...), kind=kLoop, calls=%fused_computation.21.clone.1 | loop fusion | flops 3841344 | bytes 10046592 | tf_op jit(solution)/shard_map/while/body/eval_jaxpr/mul | solution.py:59
  153.0 2.1 copy.23
  155.0 3.9 %all-to-all-start = ((f32[8,3,16,8,128]{4,0,2,1,3:T(8,128)}), f32[8,3,16,8,128]{4,0,2,1,3:T(8,128)S(1)}, u32[]{:S(2)}, u32[]{:S(2)}) async-start(f32[8,3,16,8,128]{4,0,2,1,3:T(8,128)} %copy.23), calls=%async_computation | async-start | bytes 3145728 | tf_op jit(solution)/shard_map/all_to_all | solution.py:162
  160.3 19.6 %all-to-all-done = f32[8,3,16,8,128]{4,0,2,1,3:T(8,128)S(1)} async-done(((f32[8,3,16,8,128]{4,0,2,1,3:T(8,128)}), f32[8,3,16,8,128]{4,0,2,1,3:T(8,128)S(1)}, u32[]{:S(2)}, u32[]{:S(2)}) %all-to-all-start) | async-done | bytes 1572896 | tf_op jit(solution)/shard_map/all_to_all | solution.py:162
  179.9 2.3 copy.24
  182.1 2.6 %gather_fusion = f32[256,64]{1,0:T(8,128)S(1)} fusion(f32[64,6144]{0,1:T(8,128)} %copy.24, s32[1024]{0:T(1024)S(1)} %pad_clamp_fusion), kind=kCustom, calls=%fused_computation | custom fusion | bytes 132096 | tf_op jit(solution)/shard_map/jit(_take)/gather | solution.py:90
  185.0 2.6 %collective-permute-start.3 = (f32[1,1,68,256]{3,2,1,0:T(8,128)S(1)}, f32[1,1,68,256]{3,2,1,0:T(8,128)S(1)}, u32[]{:S(2)}, u32[]{:S(2)}) collective-permute-start(f32[1,1,68,256]{3,2,1,0:T(8,128)S(1)} %bitcast.266), channel_id=1, source_target_pairs={{4,0},{8,4},{12,8},{16,12},{20,16},{24,20},{28,24},{0,28},{5,1},{9... | collective-permute-start | bytes 208904 | tf_op jit(solution)/shard_map/ppermute | solution.py:25
  187.7 2.7 %collective-permute-done.2 = f32[1,1,68,256]{3,2,1,0:T(8,128)S(1)} collective-permute-done((f32[1,1,68,256]{3,2,1,0:T(8,128)S(1)}, f32[1,1,68,256]{3,2,1,0:T(8,128)S(1)}, u32[]{:S(2)}, u32[]{:S(2)}) %collective-permute-start.2) | collective-permute-done | bytes 69664 | tf_op jit(solution)/shard_map/ppermute | solution.py:22
  194.4 6.3 %collective-permute-done.4 = f32[1,3,68,256]{3,2,1,0:T(8,128)S(1)} collective-permute-done((f32[1,3,68,256]{3,2,1,0:T(8,128)S(1)}, f32[1,3,68,256]{3,2,1,0:T(8,128)S(1)}, u32[]{:S(2)}, u32[]{:S(2)}) %collective-permute-start.4) | collective-permute-done | bytes 208928 | tf_op jit(solution)/shard_map/ppermute | solution.py:22
  200.6 2.7 %collective-permute-done.5 = f32[1,3,68,256]{3,2,1,0:T(8,128)S(1)} collective-permute-done((f32[1,3,68,256]{3,2,1,0:T(8,128)S(1)}, f32[1,3,68,256]{3,2,1,0:T(8,128)S(1)}, u32[]{:S(2)}, u32[]{:S(2)}) %collective-permute-start.5) | collective-permute-done | bytes 208928 | tf_op jit(solution)/shard_map/ppermute | solution.py:25
  219.2 23.5 %all_to_all.30 = f32[64,3,16,1,128]{4,2,1,3,0:T(8,128)S(1)} all-to-all(f32[64,3,16,1,128]{4,2,1,3,0:T(8,128)S(1)} %bitcast.263), channel_id=1, replica_groups=mesh['member'=8,'strip'=4] {'member'}, dimensions={0} | all-to-all | bytes 3145728 | tf_op jit(solution)/shard_map/all_to_all | solution.py:170
  (156 shorter events, 60.4 us)
Async XLA Ops:
  1.7 14.6 %collective-permute-start = (f32[8,3,3,1024]{3,2,0,1:T(4,128)S(1)}, f32[8,3,3,1024]{3,2,0,1:T(4,128)S(1)}, u32[]{:S(2)}, u32[]{:S(2)}) collective-permute-start(f32[8,3,3,1024]{3,2,0,1:T(4,128)S(1)} %get-tuple-element.91), channel_id=1, source_target_pairs={{1,0},{2,1},{3,2},{0,3},{5,4},{6,5},{7,6},{4,7},{9,8},{10,9},{11,1... | collective-permute-start | bytes 884744 | tf_op jit(solution)/shard_map/while/body/eval_jaxpr/ppermute | solution.py:25
  6.8 17.7 %collective-permute-start.1 = (f32[8,3,3,1024]{3,2,0,1:T(4,128)S(1)}, f32[8,3,3,1024]{3,2,0,1:T(4,128)S(1)}, u32[]{:S(2)}, u32[]{:S(2)}) collective-permute-start(f32[8,3,3,1024]{3,2,0,1:T(4,128)S(1)} %get-tuple-element.92), channel_id=1, source_target_pairs={{0,1},{1,2},{2,3},{3,0},{4,5},{5,6},{6,7},{7,4},{8,9},{9,10},{10,1... | collective-permute-start | bytes 884744 | tf_op jit(solution)/shard_map/while/body/eval_jaxpr/ppermute | solution.py:22
  24.9 1.4 copy-start
  41.8 18.5 %collective-permute-start = (f32[8,3,3,1024]{3,2,0,1:T(4,128)S(1)}, f32[8,3,3,1024]{3,2,0,1:T(4,128)S(1)}, u32[]{:S(2)}, u32[]{:S(2)}) collective-permute-start(f32[8,3,3,1024]{3,2,0,1:T(4,128)S(1)} %get-tuple-element.91), channel_id=1, source_target_pairs={{1,0},{2,1},{3,2},{0,3},{5,4},{6,5},{7,6},{4,7},{9,8},{10,9},{11,1... | collective-permute-start | bytes 884744 | tf_op jit(solution)/shard_map/while/body/eval_jaxpr/ppermute | solution.py:25
  43.6 16.7 %collective-permute-start.1 = (f32[8,3,3,1024]{3,2,0,1:T(4,128)S(1)}, f32[8,3,3,1024]{3,2,0,1:T(4,128)S(1)}, u32[]{:S(2)}, u32[]{:S(2)}) collective-permute-start(f32[8,3,3,1024]{3,2,0,1:T(4,128)S(1)} %get-tuple-element.92), channel_id=1, source_target_pairs={{0,1},{1,2},{2,3},{3,0},{4,5},{5,6},{6,7},{7,4},{8,9},{9,10},{10,1... | collective-permute-start | bytes 884744 | tf_op jit(solution)/shard_map/while/body/eval_jaxpr/ppermute | solution.py:22
  60.6 1.4 copy-start
  77.5 12.1 %collective-permute-start = (f32[8,3,3,1024]{3,2,0,1:T(4,128)S(1)}, f32[8,3,3,1024]{3,2,0,1:T(4,128)S(1)}, u32[]{:S(2)}, u32[]{:S(2)}) collective-permute-start(f32[8,3,3,1024]{3,2,0,1:T(4,128)S(1)} %get-tuple-element.91), channel_id=1, source_target_pairs={{1,0},{2,1},{3,2},{0,3},{5,4},{6,5},{7,6},{4,7},{9,8},{10,9},{11,1... | collective-permute-start | bytes 884744 | tf_op jit(solution)/shard_map/while/body/eval_jaxpr/ppermute | solution.py:25
  80.1 18.7 %collective-permute-start.1 = (f32[8,3,3,1024]{3,2,0,1:T(4,128)S(1)}, f32[8,3,3,1024]{3,2,0,1:T(4,128)S(1)}, u32[]{:S(2)}, u32[]{:S(2)}) collective-permute-start(f32[8,3,3,1024]{3,2,0,1:T(4,128)S(1)} %get-tuple-element.92), channel_id=1, source_target_pairs={{0,1},{1,2},{2,3},{3,0},{4,5},{5,6},{6,7},{7,4},{8,9},{9,10},{10,1... | collective-permute-start | bytes 884744 | tf_op jit(solution)/shard_map/while/body/eval_jaxpr/ppermute | solution.py:22
  99.2 1.4 copy-start
  116.0 11.3 %collective-permute-start = (f32[8,3,3,1024]{3,2,0,1:T(4,128)S(1)}, f32[8,3,3,1024]{3,2,0,1:T(4,128)S(1)}, u32[]{:S(2)}, u32[]{:S(2)}) collective-permute-start(f32[8,3,3,1024]{3,2,0,1:T(4,128)S(1)} %get-tuple-element.91), channel_id=1, source_target_pairs={{1,0},{2,1},{3,2},{0,3},{5,4},{6,5},{7,6},{4,7},{9,8},{10,9},{11,1... | collective-permute-start | bytes 884744 | tf_op jit(solution)/shard_map/while/body/eval_jaxpr/ppermute | solution.py:25
  117.8 17.6 %collective-permute-start.1 = (f32[8,3,3,1024]{3,2,0,1:T(4,128)S(1)}, f32[8,3,3,1024]{3,2,0,1:T(4,128)S(1)}, u32[]{:S(2)}, u32[]{:S(2)}) collective-permute-start(f32[8,3,3,1024]{3,2,0,1:T(4,128)S(1)} %get-tuple-element.92), channel_id=1, source_target_pairs={{0,1},{1,2},{2,3},{3,0},{4,5},{5,6},{6,7},{7,4},{8,9},{9,10},{10,1... | collective-permute-start | bytes 884744 | tf_op jit(solution)/shard_map/while/body/eval_jaxpr/ppermute | solution.py:22
  135.8 1.4 copy-start
  155.0 5.2 %copy-start.1 = (s32[1,1,256]{2,1,0:T(1,128)S(1)}, s32[1,1,256]{2,1,0:T(1,128)}, u32[]{:S(2)}) copy-start(s32[1,1,256]{2,1,0:T(1,128)} %param.10) | copy-start | bytes 3076
  155.0 5.2 %copy-start.3 = (f32[1,1,256]{2,1,0:T(1,128)S(1)}, f32[1,1,256]{2,1,0:T(1,128)}, u32[]{:S(2)}) copy-start(f32[1,1,256]{2,1,0:T(1,128)} %param.12) | copy-start | bytes 3076
  155.0 24.9 %all-to-all-start = ((f32[8,3,16,8,128]{4,0,2,1,3:T(8,128)}), f32[8,3,16,8,128]{4,0,2,1,3:T(8,128)S(1)}, u32[]{:S(2)}, u32[]{:S(2)}) async-start(f32[8,3,16,8,128]{4,0,2,1,3:T(8,128)} %copy.23), calls=%async_computation | async-start | bytes 3145728 | tf_op jit(solution)/shard_map/all_to_all | solution.py:162
  179.9 5.0 %copy-start.2 = (f32[1,1,256]{2,1,0:T(1,128)S(1)}, f32[1,1,256]{2,1,0:T(1,128)}, u32[]{:S(2)}) copy-start(f32[1,1,256]{2,1,0:T(1,128)} %param.11) | copy-start | bytes 3076
  184.9 5.5 %collective-permute-start.2 = (f32[1,1,68,256]{3,2,1,0:T(8,128)S(1)}, f32[1,1,68,256]{3,2,1,0:T(8,128)S(1)}, u32[]{:S(2)}, u32[]{:S(2)}) collective-permute-start(f32[1,1,68,256]{3,2,1,0:T(8,128)S(1)} %bitcast.265), channel_id=1, source_target_pairs={{0,4},{4,8},{8,12},{12,16},{16,20},{20,24},{24,28},{28,0},{1,5},{5... | collective-permute-start | bytes 208904 | tf_op jit(solution)/shard_map/ppermute | solution.py:22
  185.0 5.5 %collective-permute-start.3 = (f32[1,1,68,256]{3,2,1,0:T(8,128)S(1)}, f32[1,1,68,256]{3,2,1,0:T(8,128)S(1)}, u32[]{:S(2)}, u32[]{:S(2)}) collective-permute-start(f32[1,1,68,256]{3,2,1,0:T(8,128)S(1)} %bitcast.266), channel_id=1, source_target_pairs={{4,0},{8,4},{12,8},{16,12},{20,16},{24,20},{28,24},{0,28},{5,1},{9... | collective-permute-start | bytes 208904 | tf_op jit(solution)/shard_map/ppermute | solution.py:25
  190.5 10.2 %collective-permute-start.4 = (f32[1,3,68,256]{3,2,1,0:T(8,128)S(1)}, f32[1,3,68,256]{3,2,1,0:T(8,128)S(1)}, u32[]{:S(2)}, u32[]{:S(2)}) collective-permute-start(f32[1,3,68,256]{3,2,1,0:T(8,128)S(1)} %pad_maximum_fusion.3), channel_id=1, source_target_pairs={{0,1},{1,2},{2,3},{3,0},{4,5},{5,6},{6,7},{7,4},{8,9},{9,10},{10,1... | collective-permute-start | bytes 626696 | tf_op jit(solution)/shard_map/ppermute | solution.py:22
  192.3 11.0 %collective-permute-start.5 = (f32[1,3,68,256]{3,2,1,0:T(8,128)S(1)}, f32[1,3,68,256]{3,2,1,0:T(8,128)S(1)}, u32[]{:S(2)}, u32[]{:S(2)}) collective-permute-start(f32[1,3,68,256]{3,2,1,0:T(8,128)S(1)} %pad_maximum_fusion.3), channel_id=1, source_target_pairs={{1,0},{2,1},{3,2},{0,3},{5,4},{6,5},{7,6},{4,7},{9,8},{10,9},{11,1... | collective-permute-start | bytes 626696 | tf_op jit(solution)/shard_map/ppermute | solution.py:25
where the time goes:
time: 246 us; the launch traced here: 245 us
  waiting for transfers between devices  101 us (41%)
  other arithmetic  48.9 us (20%)
  local copies, waits for them, and re-layouts  32.3 us (13%)
  blocking collectives  23.5 us (10%)
  starting transfers between devices  22.3 us (9%)
  matrix products  13.3 us (5%)
  between operations  2.7 us (1%)
    ppermute x6, waiting for transfers between devices, with_halo(): lax.ppermute(lax.slice_in_dim(block, 0, width, axis=dim), axis, backward)  47.3 us
    ppermute x6, waiting for transfers between devices, with_halo(): lax.ppermute(lax.slice_in_dim(block, block.shape[dim] - width, None, axis...  34.5 us
    all_to_all x1, blocking collectives, on_device(): lax.all_to_all(outgoing, 'member', split_axis=0, concat_axis=3, tiled=True)  23.5 us
    mul x12, other arithmetic, advance_once(): flux_x = column_depth * flow_x  22.8 us
    all_to_all x1, waiting for transfers between devices, on_device(): lax.all_to_all(by_block, 'member', split_axis=3, concat_axis=0, tiled=True)  19.6 us
    ppermute x6, starting transfers between devices, with_halo(): lax.ppermute(lax.slice_in_dim(block, 0, width, axis=dim), axis, backward)  16 us
    mul x8, other arithmetic, advance_once(): flux_y = column_depth * flow_y  13.6 us
    concatenate x4, local copies, waits for them, and re-layouts, strip_block(): jnp.concatenate([padded[..., -halo_depth:], padded, padded[..., :halo_dep...  13 us
  transfers between devices with their start and end apart: 13, of which 11 were waited for; matrix products, arithmetic and copies ran while one was open for 0% of the time, Pallas kernels for 0%

commit v1 on v0

--- a/solution.py
+++ b/solution.py
@@ -2,6 +2,7 @@
 import jax.numpy as jnp
 from jax import lax
 from jax.sharding import PartitionSpec as P
+from jax.lax import axis_index, ppermute, psum
 
 BAND_HEIGHT_CELLS = 16
 PATCH_WIDTH_CELLS = 128
@@ -11,6 +12,25 @@
 GRAVITY = 1.0
 ROTATION = 0.05
 HIGHEST_PRECISION = lax.Precision.HIGHEST
+
+
+def sample_group(in_array, d0, join_dim):
+    front, current_arr = (psum(1, axis_name="member"), axis_index("member"))
+    side_arr = in_array.shape[d0] // front
+    lower = jnp.roll(in_array, -current_arr * side_arr, axis=d0)
+    made = [lax.slice_in_dim(lower, 0, side_arr, axis=d0)]
+    for dev in range(1, front):
+        w_next = lax.slice_in_dim(lower, dev * side_arr, (dev + 1) * side_arr, axis=d0)
+        made.append(
+            ppermute(
+                w_next,
+                axis_name="member",
+                perm=[(idx, (idx + dev) % front) for idx in range(front)],
+            )
+        )
+    z = jnp.concatenate(made[::-1], axis=join_dim)
+    carry = jnp.roll(z, shift=(current_arr + 1) * made[0].shape[join_dim], axis=join_dim)
+    return carry
 
 
 def with_halo(block, sides, width):
@@ -159,7 +179,7 @@
 
     current_state = lax.fori_loop(0, rounds, strip_round, sample_fields)
     by_block = current_state.reshape(own_members, fields, row_count, blocks, region_cols)
-    current_state = lax.all_to_all(by_block, "member", split_axis=3, concat_axis=0, tiled=True)
+    current_state = sample_group(by_block, d0=3, join_dim=0)
     region = current_state.reshape(sample_collection, fields * row_count * region_cols)
     packed = observe(
         region, report_cells[0, 0], report_values[0, 0], report_errors[0, 0], report_counts[0, 0]

time: 246 us -> 243 us (0.988)
  waiting for transfers between devices: 101 us -> 95.4 us
    all_to_all x1 -> x0, waiting for transfers between devices: 19.6 us -> none  [on_device(): lax.all_to_all(by_block, 'member', split_axis=3, concat_axis=0, tiled=True)]
    ppermute x0 -> x7, waiting for transfers between devices: none -> 13.5 us  [sample_group(): ppermute(w_next, axis_name='member', perm=[(idx, (idx + dev) % front) for...]
    ppermute x0 -> x7, starting transfers between devices: none -> 5.93 us  [sample_group(): ppermute(w_next, axis_name='member', perm=[(idx, (idx + dev) % front) for...]
    all_to_all x1 -> x0, starting transfers between devices: 3.85 us -> none  [on_device(): lax.all_to_all(by_block, 'member', split_axis=3, concat_axis=0, tiled=True)]
    ppermute x6, starting transfers between devices: 16 us -> 13.3 us  [with_halo(): lax.ppermute(lax.slice_in_dim(block, 0, width, axis=dim), axis, backward)]
  transfers between devices with their start and end apart: 13 -> 19, of which waited for: 11 -> 14; matrix products, arithmetic and copies ran while one was open for 0% -> 1% of each run, Pallas kernels for 0% -> 0%
where the time goes in v1:
time: 243 us; the launch traced here: 242 us
  waiting for transfers between devices  95.4 us (39%)
  other arithmetic  50.9 us (21%)
  local copies, waits for them, and re-layouts  31.8 us (13%)
  blocking collectives  25.3 us (10%)
  starting transfers between devices  22.3 us (9%)
  matrix products  13.3 us (5%)
  between operations  2.88 us (1%)
    ppermute x6, waiting for transfers between devices, with_halo(): lax.ppermute(lax.slice_in_dim(block, 0, width, axis=dim), axis, backward)  48.6 us
    ppermute x6, waiting for transfers between devices, with_halo(): lax.ppermute(lax.slice_in_dim(block, block.shape[dim] - width, None, axis...  33.2 us
    all_to_all x1, blocking collectives, on_device(): lax.all_to_all(outgoing, 'member', split_axis=0, concat_axis=3, tiled=True)  25.3 us
    mul x12, other arithmetic, advance_once(): flux_x = column_depth * flow_x  22.8 us
    mul x8, other arithmetic, advance_once(): flux_y = column_depth * flow_y  13.6 us
    ppermute x7, waiting for transfers between devices, sample_group(): ppermute(w_next, axis_name='member', perm=[(idx, (idx + dev) % front) for...  13.5 us
    ppermute x6, starting transfers between devices, with_halo(): lax.ppermute(lax.slice_in_dim(block, 0, width, axis=dim), axis, backward)  13.3 us
    concatenate x4, local copies, waits for them, and re-layouts, strip_block(): jnp.concatenate([padded[..., -halo_depth:], padded, padded[..., :halo_dep...  13 us
  transfers between devices with their start and end apart: 19, of which 14 were waited for; matrix products, arithmetic and copies ran while one was open for 1% of the time, Pallas kernels for 0%

profile of v1, /device:TPU:0, one launch (start us, length us, event | category | flops | bytes accessed | tf_op | source)
XLA Modules:
  0.0 242.3 jit_solution(199056094178455263)
XLA Ops:
  1.5 150.9 %while.10 = (s32[]{:T(128)}, f32[8,3,16,1024]{3,2,0,1:T(8,128)S(1)}, s32[]{:T(128)}) while((s32[]{:T(128)}, f32[8,3,16,1024]{3,2,0,1:T(8,128)S(1)}, s32[]{:T(128)}) %tuple.63), condition=%wide.region_1.0_spmd, body=%wide.region_0.0_spmd.sunk | while | flops 20949056 | bytes 80089624 | solution.py:180
  1.7 5.1 %collective-permute-start = (f32[8,3,3,1024]{3,2,0,1:T(4,128)S(1)}, f32[8,3,3,1024]{3,2,0,1:T(4,128)S(1)}, u32[]{:S(2)}, u32[]{:S(2)}) collective-permute-start(f32[8,3,3,1024]{3,2,0,1:T(4,128)S(1)} %get-tuple-element.100), channel_id=1, source_target_pairs={{1,0},{2,1},{3,2},{0,3},{5,4},{6,5},{7,6},{4,7},{9,8},{10,9},{11,1... | collective-permute-start | bytes 884744 | tf_op jit(solution)/shard_map/while/body/eval_jaxpr/ppermute | solution.py:45
  6.8 9.5 %collective-permute-done = f32[8,3,3,1024]{3,2,0,1:T(4,128)S(1)} collective-permute-done((f32[8,3,3,1024]{3,2,0,1:T(4,128)S(1)}, f32[8,3,3,1024]{3,2,0,1:T(4,128)S(1)}, u32[]{:S(2)}, u32[]{:S(2)}) %collective-permute-start) | collective-permute-done | bytes 294944 | tf_op jit(solution)/shard_map/while/body/eval_jaxpr/ppermute | solution.py:45
  16.3 8.2 %collective-permute-done.1 = f32[8,3,3,1024]{3,2,0,1:T(4,128)S(1)} collective-permute-done((f32[8,3,3,1024]{3,2,0,1:T(4,128)S(1)}, f32[8,3,3,1024]{3,2,0,1:T(4,128)S(1)}, u32[]{:S(2)}, u32[]{:S(2)}) %collective-permute-start.1) | collective-permute-done | bytes 294944 | tf_op jit(solution)/shard_map/while/body/eval_jaxpr/ppermute | solution.py:42
  26.4 3.2 %concatenate.31 = f32[8,3,22,1030]{3,2,0,1:T(8,128)S(1)} concatenate(f32[8,3,22,3]{3,2,0,1:T(8,128)S(1)} %get-tuple-element.102, f32[8,3,22,1024]{3,2,0,1:T(8,128)} %copy-done, f32[8,3,22,3]{3,2,0,1:T(8,128)S(1)} %get-tuple-element.103), dimensions={3} | concatenate | bytes 4350720 | tf_op jit(solution)/shard_map/while/body/eval_jaxpr/concatenate | solution.py:161
  29.9 2.8 %add_multiply_fusion.12 = (f32[8,20,1028]{2,1,0:T(8,128)S(1)}, f32[8,20,1028]{2,1,0:T(8,128)S(1)}, f32[8,20,1028]{2,1,0:T(8,128)S(1)}) fusion(f32[8,22,1030]{2,1,0:T(8,128)S(1)} %get-tuple-element.104, f32[8,22,1030]{2,1,0:T(8,128)S(1)} %get-tuple-element.105, f32[8,22,1030]{2,1,0:T(8,128)S(1)} %get-tuple-element.106, ...), kind=kLoop, calls=%fused_computation.23.clone.1 | loop fusion | flops 4276480 | bytes 11184640 | tf_op jit(solution)/shard_map/while/body/eval_jaxpr/mul | solution.py:79
  34.4 2.8 %add_multiply_fusion.14 = (f32[8,18,1026]{2,1,0:T(8,128)S(1)}, f32[8,18,1026]{2,1,0:T(8,128)S(1)}, f32[8,18,1026]{2,1,0:T(8,128)S(1)}) fusion(f32[8,20,1028]{2,1,0:T(8,128)S(1)} %get-tuple-element.110, f32[8,20,1028]{2,1,0:T(8,128)S(1)} %get-tuple-element.111, f32[8,20,1028]{2,1,0:T(8,128)S(1)} %get-tuple-element.109, ...), kind=kLoop, calls=%fused_computation.21.clone.1 | loop fusion | flops 3841344 | bytes 10046592 | tf_op jit(solution)/shard_map/while/body/eval_jaxpr/mul | solution.py:79
  43.8 16.4 %collective-permute-done = f32[8,3,3,1024]{3,2,0,1:T(4,128)S(1)} collective-permute-done((f32[8,3,3,1024]{3,2,0,1:T(4,128)S(1)}, f32[8,3,3,1024]{3,2,0,1:T(4,128)S(1)}, u32[]{:S(2)}, u32[]{:S(2)}) %collective-permute-start) | collective-permute-done | bytes 294944 | tf_op jit(solution)/shard_map/while/body/eval_jaxpr/ppermute | solution.py:45
  62.0 3.2 %concatenate.31 = f32[8,3,22,1030]{3,2,0,1:T(8,128)S(1)} concatenate(f32[8,3,22,3]{3,2,0,1:T(8,128)S(1)} %get-tuple-element.102, f32[8,3,22,1024]{3,2,0,1:T(8,128)} %copy-done, f32[8,3,22,3]{3,2,0,1:T(8,128)S(1)} %get-tuple-element.103), dimensions={3} | concatenate | bytes 4350720 | tf_op jit(solution)/shard_map/while/body/eval_jaxpr/concatenate | solution.py:161
  65.6 2.8 %add_multiply_fusion.12 = (f32[8,20,1028]{2,1,0:T(8,128)S(1)}, f32[8,20,1028]{2,1,0:T(8,128)S(1)}, f32[8,20,1028]{2,1,0:T(8,128)S(1)}) fusion(f32[8,22,1030]{2,1,0:T(8,128)S(1)} %get-tuple-element.104, f32[8,22,1030]{2,1,0:T(8,128)S(1)} %get-tuple-element.105, f32[8,22,1030]{2,1,0:T(8,128)S(1)} %get-tuple-element.106, ...), kind=kLoop, calls=%fused_computation.23.clone.1 | loop fusion | flops 4276480 | bytes 11184640 | tf_op jit(solution)/shard_map/while/body/eval_jaxpr/mul | solution.py:79
  70.1 2.8 %add_multiply_fusion.14 = (f32[8,18,1026]{2,1,0:T(8,128)S(1)}, f32[8,18,1026]{2,1,0:T(8,128)S(1)}, f32[8,18,1026]{2,1,0:T(8,128)S(1)}) fusion(f32[8,20,1028]{2,1,0:T(8,128)S(1)} %get-tuple-element.110, f32[8,20,1028]{2,1,0:T(8,128)S(1)} %get-tuple-element.111, f32[8,20,1028]{2,1,0:T(8,128)S(1)} %get-tuple-element.109, ...), kind=kLoop, calls=%fused_computation.21.clone.1 | loop fusion | flops 3841344 | bytes 10046592 | tf_op jit(solution)/shard_map/while/body/eval_jaxpr/mul | solution.py:79
  77.4 2.6 %collective-permute-start = (f32[8,3,3,1024]{3,2,0,1:T(4,128)S(1)}, f32[8,3,3,1024]{3,2,0,1:T(4,128)S(1)}, u32[]{:S(2)}, u32[]{:S(2)}) collective-permute-start(f32[8,3,3,1024]{3,2,0,1:T(4,128)S(1)} %get-tuple-element.100), channel_id=1, source_target_pairs={{1,0},{2,1},{3,2},{0,3},{5,4},{6,5},{7,6},{4,7},{9,8},{10,9},{11,1... | collective-permute-start | bytes 884744 | tf_op jit(solution)/shard_map/while/body/eval_jaxpr/ppermute | solution.py:45
  80.0 9.5 %collective-permute-done = f32[8,3,3,1024]{3,2,0,1:T(4,128)S(1)} collective-permute-done((f32[8,3,3,1024]{3,2,0,1:T(4,128)S(1)}, f32[8,3,3,1024]{3,2,0,1:T(4,128)S(1)}, u32[]{:S(2)}, u32[]{:S(2)}) %collective-permute-start) | collective-permute-done | bytes 294944 | tf_op jit(solution)/shard_map/while/body/eval_jaxpr/ppermute | solution.py:45
  89.5 9.2 %collective-permute-done.1 = f32[8,3,3,1024]{3,2,0,1:T(4,128)S(1)} collective-permute-done((f32[8,3,3,1024]{3,2,0,1:T(4,128)S(1)}, f32[8,3,3,1024]{3,2,0,1:T(4,128)S(1)}, u32[]{:S(2)}, u32[]{:S(2)}) %collective-permute-start.1) | collective-permute-done | bytes 294944 | tf_op jit(solution)/shard_map/while/body/eval_jaxpr/ppermute | solution.py:42
  100.5 3.2 %concatenate.31 = f32[8,3,22,1030]{3,2,0,1:T(8,128)S(1)} concatenate(f32[8,3,22,3]{3,2,0,1:T(8,128)S(1)} %get-tuple-element.102, f32[8,3,22,1024]{3,2,0,1:T(8,128)} %copy-done, f32[8,3,22,3]{3,2,0,1:T(8,128)S(1)} %get-tuple-element.103), dimensions={3} | concatenate | bytes 4350720 | tf_op jit(solution)/shard_map/while/body/eval_jaxpr/concatenate | solution.py:161
  104.1 2.8 %add_multiply_fusion.12 = (f32[8,20,1028]{2,1,0:T(8,128)S(1)}, f32[8,20,1028]{2,1,0:T(8,128)S(1)}, f32[8,20,1028]{2,1,0:T(8,128)S(1)}) fusion(f32[8,22,1030]{2,1,0:T(8,128)S(1)} %get-tuple-element.104, f32[8,22,1030]{2,1,0:T(8,128)S(1)} %get-tuple-element.105, f32[8,22,1030]{2,1,0:T(8,128)S(1)} %get-tuple-element.106, ...), kind=kLoop, calls=%fused_computation.23.clone.1 | loop fusion | flops 4276480 | bytes 11184640 | tf_op jit(solution)/shard_map/while/body/eval_jaxpr/mul | solution.py:79
  108.6 2.8 %add_multiply_fusion.14 = (f32[8,18,1026]{2,1,0:T(8,128)S(1)}, f32[8,18,1026]{2,1,0:T(8,128)S(1)}, f32[8,18,1026]{2,1,0:T(8,128)S(1)}) fusion(f32[8,20,1028]{2,1,0:T(8,128)S(1)} %get-tuple-element.110, f32[8,20,1028]{2,1,0:T(8,128)S(1)} %get-tuple-element.111, f32[8,20,1028]{2,1,0:T(8,128)S(1)} %get-tuple-element.109, ...), kind=kLoop, calls=%fused_computation.21.clone.1 | loop fusion | flops 3841344 | bytes 10046592 | tf_op jit(solution)/shard_map/while/body/eval_jaxpr/mul | solution.py:79
  117.9 9.2 %collective-permute-done = f32[8,3,3,1024]{3,2,0,1:T(4,128)S(1)} collective-permute-done((f32[8,3,3,1024]{3,2,0,1:T(4,128)S(1)}, f32[8,3,3,1024]{3,2,0,1:T(4,128)S(1)}, u32[]{:S(2)}, u32[]{:S(2)}) %collective-permute-start) | collective-permute-done | bytes 294944 | tf_op jit(solution)/shard_map/while/body/eval_jaxpr/ppermute | solution.py:45
  127.2 8.1 %collective-permute-done.1 = f32[8,3,3,1024]{3,2,0,1:T(4,128)S(1)} collective-permute-done((f32[8,3,3,1024]{3,2,0,1:T(4,128)S(1)}, f32[8,3,3,1024]{3,2,0,1:T(4,128)S(1)}, u32[]{:S(2)}, u32[]{:S(2)}) %collective-permute-start.1) | collective-permute-done | bytes 294944 | tf_op jit(solution)/shard_map/while/body/eval_jaxpr/ppermute | solution.py:42
  137.1 3.2 %concatenate.31 = f32[8,3,22,1030]{3,2,0,1:T(8,128)S(1)} concatenate(f32[8,3,22,3]{3,2,0,1:T(8,128)S(1)} %get-tuple-element.102, f32[8,3,22,1024]{3,2,0,1:T(8,128)} %copy-done, f32[8,3,22,3]{3,2,0,1:T(8,128)S(1)} %get-tuple-element.103), dimensions={3} | concatenate | bytes 4350720 | tf_op jit(solution)/shard_map/while/body/eval_jaxpr/concatenate | solution.py:161
  140.7 2.8 %add_multiply_fusion.12 = (f32[8,20,1028]{2,1,0:T(8,128)S(1)}, f32[8,20,1028]{2,1,0:T(8,128)S(1)}, f32[8,20,1028]{2,1,0:T(8,128)S(1)}) fusion(f32[8,22,1030]{2,1,0:T(8,128)S(1)} %get-tuple-element.104, f32[8,22,1030]{2,1,0:T(8,128)S(1)} %get-tuple-element.105, f32[8,22,1030]{2,1,0:T(8,128)S(1)} %get-tuple-element.106, ...), kind=kLoop, calls=%fused_computation.23.clone.1 | loop fusion | flops 4276480 | bytes 11184640 | tf_op jit(solution)/shard_map/while/body/eval_jaxpr/mul | solution.py:79
  145.1 2.8 %add_multiply_fusion.14 = (f32[8,18,1026]{2,1,0:T(8,128)S(1)}, f32[8,18,1026]{2,1,0:T(8,128)S(1)}, f32[8,18,1026]{2,1,0:T(8,128)S(1)}) fusion(f32[8,20,1028]{2,1,0:T(8,128)S(1)} %get-tuple-element.110, f32[8,20,1028]{2,1,0:T(8,128)S(1)} %get-tuple-element.111, f32[8,20,1028]{2,1,0:T(8,128)S(1)} %get-tuple-element.109, ...), kind=kLoop, calls=%fused_computation.21.clone.1 | loop fusion | flops 3841344 | bytes 10046592 | tf_op jit(solution)/shard_map/while/body/eval_jaxpr/mul | solution.py:79
  163.3 2.5 %collective-permute-done.3 = f32[8,3,16,1,128]{4,2,1,0,3:T(8,128)S(1)} collective-permute-done((f32[8,3,16,1,128]{4,2,1,0,3:T(8,128)}, f32[8,3,16,1,128]{4,2,1,0,3:T(8,128)S(1)}, u32[]{:S(2)}, u32[]{:S(2)}) %collective-permute-start.3) | collective-permute-done | bytes 196640 | tf_op jit(solution)/shard_map/ppermute | solution.py:25
  166.0 10.8 %collective-permute-done.5 = f32[8,3,16,1,128]{4,2,1,0,3:T(8,128)S(1)} collective-permute-done((f32[8,3,16,1,128]{4,2,1,0,3:T(8,128)S(1)}, f32[8,3,16,1,128]{4,2,1,0,3:T(8,128)S(1)}, u32[]{:S(2)}, u32[]{:S(2)}) %collective-permute-start.5) | collective-permute-done | bytes 196640 | tf_op jit(solution)/shard_map/ppermute | solution.py:25
  177.6 2.2 copy.27
  179.8 2.6 %gather_fusion = f32[256,64]{1,0:T(8,128)S(1)} fusion(f32[64,6144]{0,1:T(8,128)} %copy.27, s32[1024]{0:T(1024)S(1)} %pad_clamp_fusion), kind=kCustom, calls=%fused_computation | custom fusion | bytes 132096 | tf_op jit(solution)/shard_map/jit(_take)/gather | solution.py:110
  183.2 2.0 collective-permute-done.10
  185.2 2.3 collective-permute-done.9
  187.5 2.0 collective-permute-start.11
  191.4 5.5 %collective-permute-done.11 = f32[1,3,68,256]{3,2,1,0:T(8,128)S(1)} collective-permute-done((f32[1,3,68,256]{3,2,1,0:T(8,128)S(1)}, f32[1,3,68,256]{3,2,1,0:T(8,128)S(1)}, u32[]{:S(2)}, u32[]{:S(2)}) %collective-permute-start.11) | collective-permute-done | bytes 208928 | tf_op jit(solution)/shard_map/ppermute | solution.py:42
  196.9 2.0 collective-permute-done.12
  214.8 25.3 %all_to_all.15 = f32[64,3,16,1,128]{4,2,1,3,0:T(8,128)S(1)} all-to-all(f32[64,3,16,1,128]{4,2,1,3,0:T(8,128)S(1)} %bitcast.259), channel_id=1, replica_groups=mesh['member'=8,'strip'=4] {'member'}, dimensions={0} | all-to-all | bytes 3145728 | tf_op jit(solution)/shard_map/all_to_all | solution.py:190
  (189 shorter events, 68.6 us)
Async XLA Ops:
  1.7 14.6 %collective-permute-start = (f32[8,3,3,1024]{3,2,0,1:T(4,128)S(1)}, f32[8,3,3,1024]{3,2,0,1:T(4,128)S(1)}, u32[]{:S(2)}, u32[]{:S(2)}) collective-permute-start(f32[8,3,3,1024]{3,2,0,1:T(4,128)S(1)} %get-tuple-element.100), channel_id=1, source_target_pairs={{1,0},{2,1},{3,2},{0,3},{5,4},{6,5},{7,6},{4,7},{9,8},{10,9},{11,1... | collective-permute-start | bytes 884744 | tf_op jit(solution)/shard_map/while/body/eval_jaxpr/ppermute | solution.py:45
  6.8 17.7 %collective-permute-start.1 = (f32[8,3,3,1024]{3,2,0,1:T(4,128)S(1)}, f32[8,3,3,1024]{3,2,0,1:T(4,128)S(1)}, u32[]{:S(2)}, u32[]{:S(2)}) collective-permute-start(f32[8,3,3,1024]{3,2,0,1:T(4,128)S(1)} %get-tuple-element.101), channel_id=1, source_target_pairs={{0,1},{1,2},{2,3},{3,0},{4,5},{5,6},{6,7},{7,4},{8,9},{9,10},{10,1... | collective-permute-start | bytes 884744 | tf_op jit(solution)/shard_map/while/body/eval_jaxpr/ppermute | solution.py:42
  24.9 1.4 copy-start
  41.7 18.5 %collective-permute-start = (f32[8,3,3,1024]{3,2,0,1:T(4,128)S(1)}, f32[8,3,3,1024]{3,2,0,1:T(4,128)S(1)}, u32[]{:S(2)}, u32[]{:S(2)}) collective-permute-start(f32[8,3,3,1024]{3,2,0,1:T(4,128)S(1)} %get-tuple-element.100), channel_id=1, source_target_pairs={{1,0},{2,1},{3,2},{0,3},{5,4},{6,5},{7,6},{4,7},{9,8},{10,9},{11,1... | collective-permute-start | bytes 884744 | tf_op jit(solution)/shard_map/while/body/eval_jaxpr/ppermute | solution.py:45
  43.5 16.7 %collective-permute-start.1 = (f32[8,3,3,1024]{3,2,0,1:T(4,128)S(1)}, f32[8,3,3,1024]{3,2,0,1:T(4,128)S(1)}, u32[]{:S(2)}, u32[]{:S(2)}) collective-permute-start(f32[8,3,3,1024]{3,2,0,1:T(4,128)S(1)} %get-tuple-element.101), channel_id=1, source_target_pairs={{0,1},{1,2},{2,3},{3,0},{4,5},{5,6},{6,7},{7,4},{8,9},{9,10},{10,1... | collective-permute-start | bytes 884744 | tf_op jit(solution)/shard_map/while/body/eval_jaxpr/ppermute | solution.py:42
  60.6 1.4 copy-start
  77.4 12.1 %collective-permute-start = (f32[8,3,3,1024]{3,2,0,1:T(4,128)S(1)}, f32[8,3,3,1024]{3,2,0,1:T(4,128)S(1)}, u32[]{:S(2)}, u32[]{:S(2)}) collective-permute-start(f32[8,3,3,1024]{3,2,0,1:T(4,128)S(1)} %get-tuple-element.100), channel_id=1, source_target_pairs={{1,0},{2,1},{3,2},{0,3},{5,4},{6,5},{7,6},{4,7},{9,8},{10,9},{11,1... | collective-permute-start | bytes 884744 | tf_op jit(solution)/shard_map/while/body/eval_jaxpr/ppermute | solution.py:45
  80.0 18.7 %collective-permute-start.1 = (f32[8,3,3,1024]{3,2,0,1:T(4,128)S(1)}, f32[8,3,3,1024]{3,2,0,1:T(4,128)S(1)}, u32[]{:S(2)}, u32[]{:S(2)}) collective-permute-start(f32[8,3,3,1024]{3,2,0,1:T(4,128)S(1)} %get-tuple-element.101), channel_id=1, source_target_pairs={{0,1},{1,2},{2,3},{3,0},{4,5},{5,6},{6,7},{7,4},{8,9},{9,10},{10,1... | collective-permute-start | bytes 884744 | tf_op jit(solution)/shard_map/while/body/eval_jaxpr/ppermute | solution.py:42
  99.1 1.4 copy-start
  115.8 11.3 %collective-permute-start = (f32[8,3,3,1024]{3,2,0,1:T(4,128)S(1)}, f32[8,3,3,1024]{3,2,0,1:T(4,128)S(1)}, u32[]{:S(2)}, u32[]{:S(2)}) collective-permute-start(f32[8,3,3,1024]{3,2,0,1:T(4,128)S(1)} %get-tuple-element.100), channel_id=1, source_target_pairs={{1,0},{2,1},{3,2},{0,3},{5,4},{6,5},{7,6},{4,7},{9,8},{10,9},{11,1... | collective-permute-start | bytes 884744 | tf_op jit(solution)/shard_map/while/body/eval_jaxpr/ppermute | solution.py:45
  117.6 17.6 %collective-permute-start.1 = (f32[8,3,3,1024]{3,2,0,1:T(4,128)S(1)}, f32[8,3,3,1024]{3,2,0,1:T(4,128)S(1)}, u32[]{:S(2)}, u32[]{:S(2)}) collective-permute-start(f32[8,3,3,1024]{3,2,0,1:T(4,128)S(1)} %get-tuple-element.101), channel_id=1, source_target_pairs={{0,1},{1,2},{2,3},{3,0},{4,5},{5,6},{6,7},{7,4},{8,9},{9,10},{10,1... | collective-permute-start | bytes 884744 | tf_op jit(solution)/shard_map/while/body/eval_jaxpr/ppermute | solution.py:42
  135.6 1.4 copy-start
  153.1 5.6 %copy-start.1 = (s32[1,1,256]{2,1,0:T(1,128)S(1)}, s32[1,1,256]{2,1,0:T(1,128)}, u32[]{:S(2)}) copy-start(s32[1,1,256]{2,1,0:T(1,128)} %param.10) | copy-start | bytes 3076
  153.1 6.8 %copy-start.4 = (f32[1,1,256]{2,1,0:T(1,128)S(1)}, f32[1,1,256]{2,1,0:T(1,128)}, u32[]{:S(2)}) copy-start(f32[1,1,256]{2,1,0:T(1,128)} %param.12) | copy-start | bytes 3076
  154.3 7.5 %collective-permute-start.2 = (f32[8,3,16,1,128]{4,2,1,0,3:T(8,128)}, f32[8,3,16,1,128]{4,2,1,0,3:T(8,128)S(1)}, u32[]{:S(2)}, u32[]{:S(2)}) collective-permute-start(f32[8,3,16,1,128]{4,2,1,0,3:T(8,128)} %get-tuple-element.59), channel_id=1, source_target_pairs={{0,28},{4,0},{8,4},{12,8},{16,12},{20,16},{24,20},{28,24},{1,29},{... | collective-permute-start | bytes 589832 | tf_op jit(solution)/shard_map/ppermute | solution.py:25
  155.3 10.6 %collective-permute-start.3 = (f32[8,3,16,1,128]{4,2,1,0,3:T(8,128)}, f32[8,3,16,1,128]{4,2,1,0,3:T(8,128)S(1)}, u32[]{:S(2)}, u32[]{:S(2)}) collective-permute-start(f32[8,3,16,1,128]{4,2,1,0,3:T(8,128)} %get-tuple-element.58), channel_id=1, source_target_pairs={{0,24},{4,28},{8,0},{12,4},{16,8},{20,12},{24,16},{28,20},{1,25},{... | collective-permute-start | bytes 589832 | tf_op jit(solution)/shard_map/ppermute | solution.py:25
  156.7 9.3 %collective-permute-start.4 = (f32[8,3,16,1,128]{4,2,1,0,3:T(8,128)S(1)}, f32[8,3,16,1,128]{4,2,1,0,3:T(8,128)S(1)}, u32[]{:S(2)}, u32[]{:S(2)}) collective-permute-start(f32[8,3,16,1,128]{4,2,1,0,3:T(8,128)S(1)} %get-tuple-element.57), channel_id=1, source_target_pairs={{0,20},{4,24},{8,28},{12,0},{16,4},{20,8},{24,12},{28,16},{1,21},{... | collective-permute-start | bytes 589832 | tf_op jit(solution)/shard_map/ppermute | solution.py:25
  157.0 19.8 %collective-permute-start.5 = (f32[8,3,16,1,128]{4,2,1,0,3:T(8,128)S(1)}, f32[8,3,16,1,128]{4,2,1,0,3:T(8,128)S(1)}, u32[]{:S(2)}, u32[]{:S(2)}) collective-permute-start(f32[8,3,16,1,128]{4,2,1,0,3:T(8,128)S(1)} %get-tuple-element.56), channel_id=1, source_target_pairs={{0,16},{4,20},{8,24},{12,28},{16,0},{20,4},{24,8},{28,12},{1,17},{... | collective-permute-start | bytes 589832 | tf_op jit(solution)/shard_map/ppermute | solution.py:25
  158.6 18.3 %collective-permute-start.6 = (f32[8,3,16,1,128]{4,2,1,0,3:T(8,128)S(1)}, f32[8,3,16,1,128]{4,2,1,0,3:T(8,128)S(1)}, u32[]{:S(2)}, u32[]{:S(2)}) collective-permute-start(f32[8,3,16,1,128]{4,2,1,0,3:T(8,128)S(1)} %get-tuple-element.55), channel_id=1, source_target_pairs={{0,12},{4,16},{8,20},{12,24},{16,28},{20,0},{24,4},{28,8},{1,13},{... | collective-permute-start | bytes 589832 | tf_op jit(solution)/shard_map/ppermute | solution.py:25
  161.8 15.1 %collective-permute-start.7 = (f32[8,3,16,1,128]{4,2,1,0,3:T(8,128)S(1)}, f32[8,3,16,1,128]{4,2,1,0,3:T(8,128)S(1)}, u32[]{:S(2)}, u32[]{:S(2)}) collective-permute-start(f32[8,3,16,1,128]{4,2,1,0,3:T(8,128)S(1)} %get-tuple-element.54), channel_id=1, source_target_pairs={{0,8},{4,12},{8,16},{12,20},{16,24},{20,28},{24,0},{28,4},{1,9},{5... | collective-permute-start | bytes 589832 | tf_op jit(solution)/shard_map/ppermute | solution.py:25
  165.9 11.1 %collective-permute-start.8 = (f32[8,3,16,1,128]{4,2,1,0,3:T(8,128)S(1)}, f32[8,3,16,1,128]{4,2,1,0,3:T(8,128)S(1)}, u32[]{:S(2)}, u32[]{:S(2)}) collective-permute-start(f32[8,3,16,1,128]{4,2,1,0,3:T(8,128)S(1)} %get-tuple-element.53), channel_id=1, source_target_pairs={{0,4},{4,8},{8,12},{12,16},{16,20},{20,24},{24,28},{28,0},{1,5},{5... | collective-permute-start | bytes 589832 | tf_op jit(solution)/shard_map/ppermute | solution.py:25
  177.6 5.0 %copy-start.2 = (pred[256]{0:T(512)(128)(4,1)S(1)}, pred[256]{0:T(512)(128)(4,1)}, u32[]{:S(2)}) copy-start(pred[256]{0:T(512)(128)(4,1)} %compare_and_fusion) | copy-start | bytes 772
  177.6 5.0 %copy-start.3 = (f32[1,1,256]{2,1,0:T(1,128)S(1)}, f32[1,1,256]{2,1,0:T(1,128)}, u32[]{:S(2)}) copy-start(f32[1,1,256]{2,1,0:T(1,128)} %param.11) | copy-start | bytes 3076
  182.7 2.5 %collective-permute-start.10 = (f32[1,1,68,256]{3,2,1,0:T(8,128)S(1)}, f32[1,1,68,256]{3,2,1,0:T(8,128)S(1)}, u32[]{:S(2)}, u32[]{:S(2)}) collective-permute-start(f32[1,1,68,256]{3,2,1,0:T(8,128)S(1)} %bitcast.261), channel_id=1, source_target_pairs={{4,0},{8,4},{12,8},{16,12},{20,16},{24,20},{28,24},{0,28},{5,1},{9... | collective-permute-start | bytes 208904 | tf_op jit(solution)/shard_map/ppermute | solution.py:45
  182.7 4.7 %collective-permute-start.9 = (f32[1,1,68,256]{3,2,1,0:T(8,128)S(1)}, f32[1,1,68,256]{3,2,1,0:T(8,128)S(1)}, u32[]{:S(2)}, u32[]{:S(2)}) collective-permute-start(f32[1,1,68,256]{3,2,1,0:T(8,128)S(1)} %bitcast.262), channel_id=1, source_target_pairs={{0,4},{4,8},{8,12},{12,16},{16,20},{20,24},{24,28},{28,0},{1,5},{5... | collective-permute-start | bytes 208904 | tf_op jit(solution)/shard_map/ppermute | solution.py:42
  187.5 9.4 %collective-permute-start.11 = (f32[1,3,68,256]{3,2,1,0:T(8,128)S(1)}, f32[1,3,68,256]{3,2,1,0:T(8,128)S(1)}, u32[]{:S(2)}, u32[]{:S(2)}) collective-permute-start(f32[1,3,68,256]{3,2,1,0:T(8,128)S(1)} %pad_maximum_fusion.3), channel_id=1, source_target_pairs={{0,1},{1,2},{2,3},{3,0},{4,5},{5,6},{6,7},{7,4},{8,9},{9,10},{10,1... | collective-permute-start | bytes 626696 | tf_op jit(solution)/shard_map/ppermute | solution.py:42
  189.4 9.5 %collective-permute-start.12 = (f32[1,3,68,256]{3,2,1,0:T(8,128)S(1)}, f32[1,3,68,256]{3,2,1,0:T(8,128)S(1)}, u32[]{:S(2)}, u32[]{:S(2)}) collective-permute-start(f32[1,3,68,256]{3,2,1,0:T(8,128)S(1)} %pad_maximum_fusion.3), channel_id=1, source_target_pairs={{1,0},{2,1},{3,2},{0,3},{5,4},{6,5},{7,6},{4,7},{9,8},{10,9},{11,1... | collective-permute-start | bytes 626696 | tf_op jit(solution)/shard_map/ppermute | solution.py:45
